TPU v7x, 32 devices: a whole 2x2x4 slice. The times are simulated.
32 devices in a mesh: seq: 8 (over z, y), head: 4 (over x, core).
Axes of the slice: x: 2, y: 2, z: 4, core: 2. Of those that a mesh axis runs over, the one named last changes fastest.
Arguments:
- queries: bfloat16 [1024, 4096], P('seq', 'head'), may hold values from -12 to 12
- keys: bfloat16 [1024, 2048], P('seq', 'head'), may hold values from -12 to 12
- values: bfloat16 [1024, 2048], P('seq', 'head'), may hold values from -6 to 6
- block_order: int32 [16], replicated, may hold values from 0 to 15, each once
Outputs:
- attn: bfloat16 [1024, 4096], P(('seq', 'head'))
- lse: float32 [16, 1024], P('head', 'seq')
Inputs may be any that keep to these rules, and one draw needn't show every extreme that they name: device-order block j (rows j * 64 to j * 64 + 63) holds sequence positions block_order[j] * 64 onward, in order.
All inputs are finite; a program needn't handle non-finite values.
Results may differ from a plain program's by a relative error of at most 0.006.
Values may be sent and summed in bfloat16 or wider, within the bound.
A program may use at most 128 MiB of HBM per device.

v0:
```python
import jax
import jax.numpy as jnp
from jax import lax
from jax.sharding import PartitionSpec as P

HEAD_SIZE = 256
QUERY_GROUP = 2


def passed_along(block, axis, distance):
    devices = range(lax.axis_size(axis))
    route = [((i - distance) % len(devices), i) for i in devices]
    return lax.ppermute(block, axis, route)


def positions(order, first_block, count, blk):
    ids = lax.dynamic_slice_in_dim(order, first_block, count, 0)
    return (ids[:, None] * blk + jnp.arange(blk, dtype=jnp.int32)[None, :]).reshape(-1)


def attend(state, queries, keys, values, query_pos, key_pos, scale):
    maximum, total, accum = state
    scores = jnp.einsum("qhgd,khd->hgqk", queries, keys, preferred_element_type=jnp.float32) * scale
    allowed = key_pos[None, :] <= query_pos[:, None]
    scores = jnp.where(allowed, scores, -1e30)
    fresh = jnp.maximum(maximum, jnp.max(scores, axis=-1))
    weights = jnp.where(allowed, jnp.exp(scores - fresh[..., None]), 0.0)
    factor = jnp.exp(maximum - fresh)
    total = total * factor + jnp.sum(weights, axis=-1)
    update = jnp.einsum(
        "hgqk,khd->qhgd", weights.astype(jnp.bfloat16), values, preferred_element_type=jnp.float32
    )
    accum = accum * jnp.transpose(factor, (2, 0, 1))[..., None] + update
    return (fresh, total, accum)


def local(queries, keys, values, block_order):
    rows = queries.shape[0]
    blk = rows // 2
    head_dim = HEAD_SIZE
    group = QUERY_GROUP
    kv_local = keys.shape[1] // head_dim
    scale = head_dim ** (-0.5)
    my_index = lax.axis_index("seq")
    seq_count = lax.axis_size("seq")
    query_head_count = queries.reshape(rows, kv_local, group, head_dim)
    query_pos = positions(block_order, my_index * 2, 2, blk)

    def absorb(state, part_keys, part_values, key_pos, first, count):
        key_rows = part_keys.shape[0]
        sub_state = (
            state[0][first : first + count],
            state[1][first : first + count],
            state[2][:, first : first + count],
        )
        sub_queries = query_head_count[:, first : first + count]
        key_heads = part_keys.reshape(key_rows, count, head_dim)
        value_heads = part_values.reshape(key_rows, count, head_dim)
        sub_state = attend(
            sub_state, sub_queries, key_heads, value_heads, query_pos, key_pos, scale
        )
        return (
            state[0].at[first : first + count].set(sub_state[0]),
            state[1].at[first : first + count].set(sub_state[1]),
            state[2].at[:, first : first + count].set(sub_state[2]),
        )

    initial = (
        jnp.full((kv_local, group, rows), -1e30, jnp.float32),
        jnp.zeros((kv_local, group, rows), jnp.float32),
        jnp.zeros((rows, kv_local, group, head_dim), jnp.float32),
    )
    half_heads = kv_local // 2
    width = half_heads * head_dim
    state = absorb(initial, keys, values, query_pos, 0, kv_local)

    def both_turn(step, carry):
        current, ahead_keys, ahead_values, behind_keys, behind_values = carry
        ahead_keys, ahead_values = passed_along((ahead_keys, ahead_values), "seq", 1)
        behind_keys, behind_values = passed_along((behind_keys, behind_values), "seq", -1)
        source_ahead = (my_index - step) % seq_count
        source_behind = (my_index + step) % seq_count
        current = absorb(
            current,
            ahead_keys,
            ahead_values,
            positions(block_order, source_ahead * 2, 2, blk),
            0,
            half_heads,
        )
        current = absorb(
            current,
            behind_keys,
            behind_values,
            positions(block_order, source_behind * 2, 2, blk),
            half_heads,
            half_heads,
        )
        return (current, ahead_keys, ahead_values, behind_keys, behind_values)

    state = lax.fori_loop(
        1,
        seq_count,
        both_turn,
        (state, keys[:, :width], values[:, :width], keys[:, width:], values[:, width:]),
    )[0]
    maximum, total, accum = state
    output = accum / jnp.transpose(total, (2, 0, 1))[..., None]
    output = output.reshape(rows, kv_local * group * head_dim).astype(jnp.bfloat16)
    lse = (maximum + jnp.log(total)).reshape(kv_local * group, rows)
    attn = lax.all_to_all(output, "head", split_axis=0, concat_axis=1, tiled=True)
    return (attn, lse)


def solution(mesh):
    in_specs = (P("seq", "head"), P("seq", "head"), P("seq", "head"), P())
    out_specs = (P(("seq", "head"), None), P("head", "seq"))
    return jax.shard_map(local, mesh=mesh, in_specs=in_specs, out_specs=out_specs, check_vma=False)
```

profile of v0, /device:TPU:0, one launch (start us, length us, event | category | flops | bytes accessed | tf_op | source)
XLA Modules:
  0.0 90.0 jit_solution(7113694675955241974)
XLA Ops:
  0.6 1.0 %reshape.722 = bf16[128,2,256]{2,1,0:T(2,128)(2,1)S(1)} reshape(bf16[128,512]{1,0:T(8,128)(2,1)} %param.31) | data formatting | bytes 262144 | tf_op jit(solution)/shard_map/reshape | solution.py:57
  1.7 0.9 copy-done
  4.5 74.0 %while.41 = (s32[]{:T(128)}, f32[2,2,128]{2,1,0:T(2,128)S(1)}, f32[2,2,128]{2,1,0:T(2,128)S(1)}, f32[128,2,2,256]{3,0,2,1:T(8,128)S(1)}, bf16[128,256]{1,0:T(8,1...) while((s32[]{:T(128)}, f32[2,2,128]{2,1,0:T(2,128)S(1)}, ...), condition=%wide.region_7.8_spmd.clone, body=%wide.region_2.7_spmd.clone.sunk | while | flops 67995552 | bytes 4100819 | solution.py:101
  4.5 3.0 %collective-permute-start = (bf16[128,256]{1,0:T(8,128)(2,1)S(1)}, bf16[128,256]{1,0:T(8,128)(2,1)S(1)}, u32[]{:S(2)}, u32[]{:S(2)}) collective-permute-start(bf16[128,256]{1,0:T(8,128)(2,1)S(1)} %get-tuple-element.767), channel_id=1, source_target_pairs={{28,0},{0,4},{4,8},{8,12},{12,16},{16,20},{20,24},{24,28},{29,1},{... | collective-permute-start | bytes 196616 | tf_op jit(solution)/shard_map/while/body/eval_jaxpr/ppermute | solution.py:13
  7.6 1.5 %collective-permute-start.2 = (bf16[128,256]{1,0:T(8,128)(2,1)S(1)}, bf16[128,256]{1,0:T(8,128)(2,1)S(1)}, u32[]{:S(2)}, u32[]{:S(2)}) collective-permute-start(bf16[128,256]{1,0:T(8,128)(2,1)S(1)} %get-tuple-element.768), channel_id=1, source_target_pairs={{28,0},{0,4},{4,8},{8,12},{12,16},{16,20},{20,24},{24,28},{29,1},{... | collective-permute-start | bytes 196616 | tf_op jit(solution)/shard_map/while/body/eval_jaxpr/ppermute | solution.py:13
  9.1 3.2 %collective-permute-start.1 = (bf16[128,256]{1,0:T(8,128)(2,1)S(1)}, bf16[128,256]{1,0:T(8,128)(2,1)S(1)}, u32[]{:S(2)}, u32[]{:S(2)}) collective-permute-start(bf16[128,256]{1,0:T(8,128)(2,1)S(1)} %get-tuple-element.769), channel_id=1, source_target_pairs={{4,0},{8,4},{12,8},{16,12},{20,16},{24,20},{28,24},{0,28},{5,1},{9... | collective-permute-start | bytes 196616 | tf_op jit(solution)/shard_map/while/body/eval_jaxpr/ppermute | solution.py:13
  13.6 2.1 %collective-permute-done.1 = bf16[128,256]{1,0:T(8,128)(2,1)S(1)} collective-permute-done((bf16[128,256]{1,0:T(8,128)(2,1)S(1)}, bf16[128,256]{1,0:T(8,128)(2,1)S(1)}, u32[]{:S(2)}, u32[]{:S(2)}) %collective-permute-start.1) | collective-permute-done | bytes 65568 | tf_op jit(solution)/shard_map/while/body/eval_jaxpr/ppermute | solution.py:13
  17.3 1.9 %collective-permute-start.2 = (bf16[128,256]{1,0:T(8,128)(2,1)S(1)}, bf16[128,256]{1,0:T(8,128)(2,1)S(1)}, u32[]{:S(2)}, u32[]{:S(2)}) collective-permute-start(bf16[128,256]{1,0:T(8,128)(2,1)S(1)} %get-tuple-element.768), channel_id=1, source_target_pairs={{28,0},{0,4},{4,8},{8,12},{12,16},{16,20},{20,24},{24,28},{29,1},{... | collective-permute-start | bytes 196616 | tf_op jit(solution)/shard_map/while/body/eval_jaxpr/ppermute | solution.py:13
  19.1 2.9 %collective-permute-start.1 = (bf16[128,256]{1,0:T(8,128)(2,1)S(1)}, bf16[128,256]{1,0:T(8,128)(2,1)S(1)}, u32[]{:S(2)}, u32[]{:S(2)}) collective-permute-start(bf16[128,256]{1,0:T(8,128)(2,1)S(1)} %get-tuple-element.769), channel_id=1, source_target_pairs={{4,0},{8,4},{12,8},{16,12},{20,16},{24,20},{28,24},{0,28},{5,1},{9... | collective-permute-start | bytes 196616 | tf_op jit(solution)/shard_map/while/body/eval_jaxpr/ppermute | solution.py:13
  22.0 2.0 %collective-permute-start.3 = (bf16[128,256]{1,0:T(8,128)(2,1)S(1)}, bf16[128,256]{1,0:T(8,128)(2,1)S(1)}, u32[]{:S(2)}, u32[]{:S(2)}) collective-permute-start(bf16[128,256]{1,0:T(8,128)(2,1)S(1)} %get-tuple-element.770), channel_id=1, source_target_pairs={{4,0},{8,4},{12,8},{16,12},{20,16},{24,20},{28,24},{0,28},{5,1},{9... | collective-permute-start | bytes 196616 | tf_op jit(solution)/shard_map/while/body/eval_jaxpr/ppermute | solution.py:13
  24.9 1.1 %collective-permute-done.1 = bf16[128,256]{1,0:T(8,128)(2,1)S(1)} collective-permute-done((bf16[128,256]{1,0:T(8,128)(2,1)S(1)}, bf16[128,256]{1,0:T(8,128)(2,1)S(1)}, u32[]{:S(2)}, u32[]{:S(2)}) %collective-permute-start.1) | collective-permute-done | bytes 65568 | tf_op jit(solution)/shard_map/while/body/eval_jaxpr/ppermute | solution.py:13
  27.5 1.4 %collective-permute-start.2 = (bf16[128,256]{1,0:T(8,128)(2,1)S(1)}, bf16[128,256]{1,0:T(8,128)(2,1)S(1)}, u32[]{:S(2)}, u32[]{:S(2)}) collective-permute-start(bf16[128,256]{1,0:T(8,128)(2,1)S(1)} %get-tuple-element.768), channel_id=1, source_target_pairs={{28,0},{0,4},{4,8},{8,12},{12,16},{16,20},{20,24},{24,28},{29,1},{... | collective-permute-start | bytes 196616 | tf_op jit(solution)/shard_map/while/body/eval_jaxpr/ppermute | solution.py:13
  28.9 3.4 %collective-permute-start.1 = (bf16[128,256]{1,0:T(8,128)(2,1)S(1)}, bf16[128,256]{1,0:T(8,128)(2,1)S(1)}, u32[]{:S(2)}, u32[]{:S(2)}) collective-permute-start(bf16[128,256]{1,0:T(8,128)(2,1)S(1)} %get-tuple-element.769), channel_id=1, source_target_pairs={{4,0},{8,4},{12,8},{16,12},{20,16},{24,20},{28,24},{0,28},{5,1},{9... | collective-permute-start | bytes 196616 | tf_op jit(solution)/shard_map/while/body/eval_jaxpr/ppermute | solution.py:13
  32.3 2.0 %collective-permute-start.3 = (bf16[128,256]{1,0:T(8,128)(2,1)S(1)}, bf16[128,256]{1,0:T(8,128)(2,1)S(1)}, u32[]{:S(2)}, u32[]{:S(2)}) collective-permute-start(bf16[128,256]{1,0:T(8,128)(2,1)S(1)} %get-tuple-element.770), channel_id=1, source_target_pairs={{4,0},{8,4},{12,8},{16,12},{20,16},{24,20},{28,24},{0,28},{5,1},{9... | collective-permute-start | bytes 196616 | tf_op jit(solution)/shard_map/while/body/eval_jaxpr/ppermute | solution.py:13
  35.2 1.3 %collective-permute-done.1 = bf16[128,256]{1,0:T(8,128)(2,1)S(1)} collective-permute-done((bf16[128,256]{1,0:T(8,128)(2,1)S(1)}, bf16[128,256]{1,0:T(8,128)(2,1)S(1)}, u32[]{:S(2)}, u32[]{:S(2)}) %collective-permute-start.1) | collective-permute-done | bytes 65568 | tf_op jit(solution)/shard_map/while/body/eval_jaxpr/ppermute | solution.py:13
  38.5 4.2 %collective-permute-start.1 = (bf16[128,256]{1,0:T(8,128)(2,1)S(1)}, bf16[128,256]{1,0:T(8,128)(2,1)S(1)}, u32[]{:S(2)}, u32[]{:S(2)}) collective-permute-start(bf16[128,256]{1,0:T(8,128)(2,1)S(1)} %get-tuple-element.769), channel_id=1, source_target_pairs={{4,0},{8,4},{12,8},{16,12},{20,16},{24,20},{28,24},{0,28},{5,1},{9... | collective-permute-start | bytes 196616 | tf_op jit(solution)/shard_map/while/body/eval_jaxpr/ppermute | solution.py:13
  42.7 2.0 %collective-permute-start.3 = (bf16[128,256]{1,0:T(8,128)(2,1)S(1)}, bf16[128,256]{1,0:T(8,128)(2,1)S(1)}, u32[]{:S(2)}, u32[]{:S(2)}) collective-permute-start(bf16[128,256]{1,0:T(8,128)(2,1)S(1)} %get-tuple-element.770), channel_id=1, source_target_pairs={{4,0},{8,4},{12,8},{16,12},{20,16},{24,20},{28,24},{0,28},{5,1},{9... | collective-permute-start | bytes 196616 | tf_op jit(solution)/shard_map/while/body/eval_jaxpr/ppermute | solution.py:13
  45.9 1.0 %collective-permute-done.3 = bf16[128,256]{1,0:T(8,128)(2,1)S(1)} collective-permute-done((bf16[128,256]{1,0:T(8,128)(2,1)S(1)}, bf16[128,256]{1,0:T(8,128)(2,1)S(1)}, u32[]{:S(2)}, u32[]{:S(2)}) %collective-permute-start.3) | collective-permute-done | bytes 65568 | tf_op jit(solution)/shard_map/while/body/eval_jaxpr/ppermute | solution.py:13
  47.9 4.6 %collective-permute-start.1 = (bf16[128,256]{1,0:T(8,128)(2,1)S(1)}, bf16[128,256]{1,0:T(8,128)(2,1)S(1)}, u32[]{:S(2)}, u32[]{:S(2)}) collective-permute-start(bf16[128,256]{1,0:T(8,128)(2,1)S(1)} %get-tuple-element.769), channel_id=1, source_target_pairs={{4,0},{8,4},{12,8},{16,12},{20,16},{24,20},{28,24},{0,28},{5,1},{9... | collective-permute-start | bytes 196616 | tf_op jit(solution)/shard_map/while/body/eval_jaxpr/ppermute | solution.py:13
  52.4 2.0 %collective-permute-start.3 = (bf16[128,256]{1,0:T(8,128)(2,1)S(1)}, bf16[128,256]{1,0:T(8,128)(2,1)S(1)}, u32[]{:S(2)}, u32[]{:S(2)}) collective-permute-start(bf16[128,256]{1,0:T(8,128)(2,1)S(1)} %get-tuple-element.770), channel_id=1, source_target_pairs={{4,0},{8,4},{12,8},{16,12},{20,16},{24,20},{28,24},{0,28},{5,1},{9... | collective-permute-start | bytes 196616 | tf_op jit(solution)/shard_map/while/body/eval_jaxpr/ppermute | solution.py:13
  55.3 1.1 %collective-permute-done.1 = bf16[128,256]{1,0:T(8,128)(2,1)S(1)} collective-permute-done((bf16[128,256]{1,0:T(8,128)(2,1)S(1)}, bf16[128,256]{1,0:T(8,128)(2,1)S(1)}, u32[]{:S(2)}, u32[]{:S(2)}) %collective-permute-start.1) | collective-permute-done | bytes 65568 | tf_op jit(solution)/shard_map/while/body/eval_jaxpr/ppermute | solution.py:13
  57.9 0.7 collective-permute-start.2
  58.6 4.0 %collective-permute-start.1 = (bf16[128,256]{1,0:T(8,128)(2,1)S(1)}, bf16[128,256]{1,0:T(8,128)(2,1)S(1)}, u32[]{:S(2)}, u32[]{:S(2)}) collective-permute-start(bf16[128,256]{1,0:T(8,128)(2,1)S(1)} %get-tuple-element.769), channel_id=1, source_target_pairs={{4,0},{8,4},{12,8},{16,12},{20,16},{24,20},{28,24},{0,28},{5,1},{9... | collective-permute-start | bytes 196616 | tf_op jit(solution)/shard_map/while/body/eval_jaxpr/ppermute | solution.py:13
  62.7 2.0 %collective-permute-start.3 = (bf16[128,256]{1,0:T(8,128)(2,1)S(1)}, bf16[128,256]{1,0:T(8,128)(2,1)S(1)}, u32[]{:S(2)}, u32[]{:S(2)}) collective-permute-start(bf16[128,256]{1,0:T(8,128)(2,1)S(1)} %get-tuple-element.770), channel_id=1, source_target_pairs={{4,0},{8,4},{12,8},{16,12},{20,16},{24,20},{28,24},{0,28},{5,1},{9... | collective-permute-start | bytes 196616 | tf_op jit(solution)/shard_map/while/body/eval_jaxpr/ppermute | solution.py:13
  65.5 1.1 %collective-permute-done.1 = bf16[128,256]{1,0:T(8,128)(2,1)S(1)} collective-permute-done((bf16[128,256]{1,0:T(8,128)(2,1)S(1)}, bf16[128,256]{1,0:T(8,128)(2,1)S(1)}, u32[]{:S(2)}, u32[]{:S(2)}) %collective-permute-start.1) | collective-permute-done | bytes 65568 | tf_op jit(solution)/shard_map/while/body/eval_jaxpr/ppermute | solution.py:13
  68.2 0.7 collective-permute-start.2
  69.0 4.0 %collective-permute-start.1 = (bf16[128,256]{1,0:T(8,128)(2,1)S(1)}, bf16[128,256]{1,0:T(8,128)(2,1)S(1)}, u32[]{:S(2)}, u32[]{:S(2)}) collective-permute-start(bf16[128,256]{1,0:T(8,128)(2,1)S(1)} %get-tuple-element.769), channel_id=1, source_target_pairs={{4,0},{8,4},{12,8},{16,12},{20,16},{24,20},{28,24},{0,28},{5,1},{9... | collective-permute-start | bytes 196616 | tf_op jit(solution)/shard_map/while/body/eval_jaxpr/ppermute | solution.py:13
  73.0 2.0 %collective-permute-start.3 = (bf16[128,256]{1,0:T(8,128)(2,1)S(1)}, bf16[128,256]{1,0:T(8,128)(2,1)S(1)}, u32[]{:S(2)}, u32[]{:S(2)}) collective-permute-start(bf16[128,256]{1,0:T(8,128)(2,1)S(1)} %get-tuple-element.770), channel_id=1, source_target_pairs={{4,0},{8,4},{12,8},{16,12},{20,16},{24,20},{28,24},{0,28},{5,1},{9... | collective-permute-start | bytes 196616 | tf_op jit(solution)/shard_map/while/body/eval_jaxpr/ppermute | solution.py:13
  75.9 1.2 %collective-permute-done.1 = bf16[128,256]{1,0:T(8,128)(2,1)S(1)} collective-permute-done((bf16[128,256]{1,0:T(8,128)(2,1)S(1)}, bf16[128,256]{1,0:T(8,128)(2,1)S(1)}, u32[]{:S(2)}, u32[]{:S(2)}) %collective-permute-start.1) | collective-permute-done | bytes 65568 | tf_op jit(solution)/shard_map/while/body/eval_jaxpr/ppermute | solution.py:13
  79.0 0.9 convert_element_type.34
  79.9 3.4 %all-to-all-start = ((bf16[4,32,1024]{2,1,0:T(8,128)(2,1)}), bf16[4,32,1024]{2,1,0:T(8,128)(2,1)S(1)}, u32[]{:S(2)}, u32[]{:S(2)}) async-start(bf16[4,32,1024]{2,1,0:T(8,128)(2,1)} %convert_element_type.34), calls=%async_computation | async-start | bytes 524288 | tf_op jit(solution)/shard_map/all_to_all | solution.py:111
  83.9 5.4 %all-to-all-done = bf16[4,32,1024]{2,1,0:T(8,128)(2,1)S(1)} async-done(((bf16[4,32,1024]{2,1,0:T(8,128)(2,1)}), bf16[4,32,1024]{2,1,0:T(8,128)(2,1)S(1)}, u32[]{:S(2)}, u32[]{:S(2)}) %all-to-all-start) | async-done | bytes 262176 | tf_op jit(solution)/shard_map/all_to_all | solution.py:111
  (201 shorter events, 20.5 us)
Async XLA Ops:
  0.6 1.0 %copy-start.1 = (bf16[128,512]{1,0:T(8,128)(2,1)S(1)}, bf16[128,512]{1,0:T(8,128)(2,1)}, u32[]{:S(2)}) copy-start(bf16[128,512]{1,0:T(8,128)(2,1)} %param.32) | copy-start | bytes 393220
  1.6 0.9 %copy-start = (bf16[128,512]{1,0:T(8,128)(2,1)S(1)}, bf16[128,512]{1,0:T(8,128)(2,1)}, u32[]{:S(2)}) copy-start(bf16[128,512]{1,0:T(8,128)(2,1)} %param.31) | copy-start | bytes 393220
  2.5 1.1 %copy-start.2 = (bf16[128,1024]{1,0:T(8,128)(2,1)S(1)}, bf16[128,1024]{1,0:T(8,128)(2,1)}, u32[]{:S(2)}) copy-start(bf16[128,1024]{1,0:T(8,128)(2,1)} %param.30) | copy-start | bytes 786436
  4.5 8.8 %collective-permute-start = (bf16[128,256]{1,0:T(8,128)(2,1)S(1)}, bf16[128,256]{1,0:T(8,128)(2,1)S(1)}, u32[]{:S(2)}, u32[]{:S(2)}) collective-permute-start(bf16[128,256]{1,0:T(8,128)(2,1)S(1)} %get-tuple-element.767), channel_id=1, source_target_pairs={{28,0},{0,4},{4,8},{8,12},{12,16},{16,20},{20,24},{24,28},{29,1},{... | collective-permute-start | bytes 196616 | tf_op jit(solution)/shard_map/while/body/eval_jaxpr/ppermute | solution.py:13
  7.6 8.4 %collective-permute-start.2 = (bf16[128,256]{1,0:T(8,128)(2,1)S(1)}, bf16[128,256]{1,0:T(8,128)(2,1)S(1)}, u32[]{:S(2)}, u32[]{:S(2)}) collective-permute-start(bf16[128,256]{1,0:T(8,128)(2,1)S(1)} %get-tuple-element.768), channel_id=1, source_target_pairs={{28,0},{0,4},{4,8},{8,12},{12,16},{16,20},{20,24},{24,28},{29,1},{... | collective-permute-start | bytes 196616 | tf_op jit(solution)/shard_map/while/body/eval_jaxpr/ppermute | solution.py:13
  9.1 6.6 %collective-permute-start.1 = (bf16[128,256]{1,0:T(8,128)(2,1)S(1)}, bf16[128,256]{1,0:T(8,128)(2,1)S(1)}, u32[]{:S(2)}, u32[]{:S(2)}) collective-permute-start(bf16[128,256]{1,0:T(8,128)(2,1)S(1)} %get-tuple-element.769), channel_id=1, source_target_pairs={{4,0},{8,4},{12,8},{16,12},{20,16},{24,20},{28,24},{0,28},{5,1},{9... | collective-permute-start | bytes 196616 | tf_op jit(solution)/shard_map/while/body/eval_jaxpr/ppermute | solution.py:13
  12.3 4.3 %collective-permute-start.3 = (bf16[128,256]{1,0:T(8,128)(2,1)S(1)}, bf16[128,256]{1,0:T(8,128)(2,1)S(1)}, u32[]{:S(2)}, u32[]{:S(2)}) collective-permute-start(bf16[128,256]{1,0:T(8,128)(2,1)S(1)} %get-tuple-element.770), channel_id=1, source_target_pairs={{4,0},{8,4},{12,8},{16,12},{20,16},{24,20},{28,24},{0,28},{5,1},{9... | collective-permute-start | bytes 196616 | tf_op jit(solution)/shard_map/while/body/eval_jaxpr/ppermute | solution.py:13
  17.2 7.4 %collective-permute-start = (bf16[128,256]{1,0:T(8,128)(2,1)S(1)}, bf16[128,256]{1,0:T(8,128)(2,1)S(1)}, u32[]{:S(2)}, u32[]{:S(2)}) collective-permute-start(bf16[128,256]{1,0:T(8,128)(2,1)S(1)} %get-tuple-element.767), channel_id=1, source_target_pairs={{28,0},{0,4},{4,8},{8,12},{12,16},{16,20},{20,24},{24,28},{29,1},{... | collective-permute-start | bytes 196616 | tf_op jit(solution)/shard_map/while/body/eval_jaxpr/ppermute | solution.py:13
  17.3 9.1 %collective-permute-start.2 = (bf16[128,256]{1,0:T(8,128)(2,1)S(1)}, bf16[128,256]{1,0:T(8,128)(2,1)S(1)}, u32[]{:S(2)}, u32[]{:S(2)}) collective-permute-start(bf16[128,256]{1,0:T(8,128)(2,1)S(1)} %get-tuple-element.768), channel_id=1, source_target_pairs={{28,0},{0,4},{4,8},{8,12},{12,16},{16,20},{20,24},{24,28},{29,1},{... | collective-permute-start | bytes 196616 | tf_op jit(solution)/shard_map/while/body/eval_jaxpr/ppermute | solution.py:13
  19.1 6.9 %collective-permute-start.1 = (bf16[128,256]{1,0:T(8,128)(2,1)S(1)}, bf16[128,256]{1,0:T(8,128)(2,1)S(1)}, u32[]{:S(2)}, u32[]{:S(2)}) collective-permute-start(bf16[128,256]{1,0:T(8,128)(2,1)S(1)} %get-tuple-element.769), channel_id=1, source_target_pairs={{4,0},{8,4},{12,8},{16,12},{20,16},{24,20},{28,24},{0,28},{5,1},{9... | collective-permute-start | bytes 196616 | tf_op jit(solution)/shard_map/while/body/eval_jaxpr/ppermute | solution.py:13
  22.0 4.8 %collective-permute-start.3 = (bf16[128,256]{1,0:T(8,128)(2,1)S(1)}, bf16[128,256]{1,0:T(8,128)(2,1)S(1)}, u32[]{:S(2)}, u32[]{:S(2)}) collective-permute-start(bf16[128,256]{1,0:T(8,128)(2,1)S(1)} %get-tuple-element.770), channel_id=1, source_target_pairs={{4,0},{8,4},{12,8},{16,12},{20,16},{24,20},{28,24},{0,28},{5,1},{9... | collective-permute-start | bytes 196616 | tf_op jit(solution)/shard_map/while/body/eval_jaxpr/ppermute | solution.py:13
  27.5 7.4 %collective-permute-start = (bf16[128,256]{1,0:T(8,128)(2,1)S(1)}, bf16[128,256]{1,0:T(8,128)(2,1)S(1)}, u32[]{:S(2)}, u32[]{:S(2)}) collective-permute-start(bf16[128,256]{1,0:T(8,128)(2,1)S(1)} %get-tuple-element.767), channel_id=1, source_target_pairs={{28,0},{0,4},{4,8},{8,12},{12,16},{16,20},{20,24},{24,28},{29,1},{... | collective-permute-start | bytes 196616 | tf_op jit(solution)/shard_map/while/body/eval_jaxpr/ppermute | solution.py:13
  27.5 9.3 %collective-permute-start.2 = (bf16[128,256]{1,0:T(8,128)(2,1)S(1)}, bf16[128,256]{1,0:T(8,128)(2,1)S(1)}, u32[]{:S(2)}, u32[]{:S(2)}) collective-permute-start(bf16[128,256]{1,0:T(8,128)(2,1)S(1)} %get-tuple-element.768), channel_id=1, source_target_pairs={{28,0},{0,4},{4,8},{8,12},{12,16},{16,20},{20,24},{24,28},{29,1},{... | collective-permute-start | bytes 196616 | tf_op jit(solution)/shard_map/while/body/eval_jaxpr/ppermute | solution.py:13
  28.9 7.6 %collective-permute-start.1 = (bf16[128,256]{1,0:T(8,128)(2,1)S(1)}, bf16[128,256]{1,0:T(8,128)(2,1)S(1)}, u32[]{:S(2)}, u32[]{:S(2)}) collective-permute-start(bf16[128,256]{1,0:T(8,128)(2,1)S(1)} %get-tuple-element.769), channel_id=1, source_target_pairs={{4,0},{8,4},{12,8},{16,12},{20,16},{24,20},{28,24},{0,28},{5,1},{9... | collective-permute-start | bytes 196616 | tf_op jit(solution)/shard_map/while/body/eval_jaxpr/ppermute | solution.py:13
  32.3 5.0 %collective-permute-start.3 = (bf16[128,256]{1,0:T(8,128)(2,1)S(1)}, bf16[128,256]{1,0:T(8,128)(2,1)S(1)}, u32[]{:S(2)}, u32[]{:S(2)}) collective-permute-start(bf16[128,256]{1,0:T(8,128)(2,1)S(1)} %get-tuple-element.770), channel_id=1, source_target_pairs={{4,0},{8,4},{12,8},{16,12},{20,16},{24,20},{28,24},{0,28},{5,1},{9... | collective-permute-start | bytes 196616 | tf_op jit(solution)/shard_map/while/body/eval_jaxpr/ppermute | solution.py:13
  37.9 7.4 %collective-permute-start = (bf16[128,256]{1,0:T(8,128)(2,1)S(1)}, bf16[128,256]{1,0:T(8,128)(2,1)S(1)}, u32[]{:S(2)}, u32[]{:S(2)}) collective-permute-start(bf16[128,256]{1,0:T(8,128)(2,1)S(1)} %get-tuple-element.767), channel_id=1, source_target_pairs={{28,0},{0,4},{4,8},{8,12},{12,16},{16,20},{20,24},{24,28},{29,1},{... | collective-permute-start | bytes 196616 | tf_op jit(solution)/shard_map/while/body/eval_jaxpr/ppermute | solution.py:13
  37.9 8.0 %collective-permute-start.2 = (bf16[128,256]{1,0:T(8,128)(2,1)S(1)}, bf16[128,256]{1,0:T(8,128)(2,1)S(1)}, u32[]{:S(2)}, u32[]{:S(2)}) collective-permute-start(bf16[128,256]{1,0:T(8,128)(2,1)S(1)} %get-tuple-element.768), channel_id=1, source_target_pairs={{28,0},{0,4},{4,8},{8,12},{12,16},{16,20},{20,24},{24,28},{29,1},{... | collective-permute-start | bytes 196616 | tf_op jit(solution)/shard_map/while/body/eval_jaxpr/ppermute | solution.py:13
  38.5 7.1 %collective-permute-start.1 = (bf16[128,256]{1,0:T(8,128)(2,1)S(1)}, bf16[128,256]{1,0:T(8,128)(2,1)S(1)}, u32[]{:S(2)}, u32[]{:S(2)}) collective-permute-start(bf16[128,256]{1,0:T(8,128)(2,1)S(1)} %get-tuple-element.769), channel_id=1, source_target_pairs={{4,0},{8,4},{12,8},{16,12},{20,16},{24,20},{28,24},{0,28},{5,1},{9... | collective-permute-start | bytes 196616 | tf_op jit(solution)/shard_map/while/body/eval_jaxpr/ppermute | solution.py:13
  42.7 4.3 %collective-permute-start.3 = (bf16[128,256]{1,0:T(8,128)(2,1)S(1)}, bf16[128,256]{1,0:T(8,128)(2,1)S(1)}, u32[]{:S(2)}, u32[]{:S(2)}) collective-permute-start(bf16[128,256]{1,0:T(8,128)(2,1)S(1)} %get-tuple-element.770), channel_id=1, source_target_pairs={{4,0},{8,4},{12,8},{16,12},{20,16},{24,20},{28,24},{0,28},{5,1},{9... | collective-permute-start | bytes 196616 | tf_op jit(solution)/shard_map/while/body/eval_jaxpr/ppermute | solution.py:13
  47.6 7.4 %collective-permute-start = (bf16[128,256]{1,0:T(8,128)(2,1)S(1)}, bf16[128,256]{1,0:T(8,128)(2,1)S(1)}, u32[]{:S(2)}, u32[]{:S(2)}) collective-permute-start(bf16[128,256]{1,0:T(8,128)(2,1)S(1)} %get-tuple-element.767), channel_id=1, source_target_pairs={{28,0},{0,4},{4,8},{8,12},{12,16},{16,20},{20,24},{24,28},{29,1},{... | collective-permute-start | bytes 196616 | tf_op jit(solution)/shard_map/while/body/eval_jaxpr/ppermute | solution.py:13
  47.7 9.1 %collective-permute-start.2 = (bf16[128,256]{1,0:T(8,128)(2,1)S(1)}, bf16[128,256]{1,0:T(8,128)(2,1)S(1)}, u32[]{:S(2)}, u32[]{:S(2)}) collective-permute-start(bf16[128,256]{1,0:T(8,128)(2,1)S(1)} %get-tuple-element.768), channel_id=1, source_target_pairs={{28,0},{0,4},{4,8},{8,12},{12,16},{16,20},{20,24},{24,28},{29,1},{... | collective-permute-start | bytes 196616 | tf_op jit(solution)/shard_map/while/body/eval_jaxpr/ppermute | solution.py:13
  47.9 8.5 %collective-permute-start.1 = (bf16[128,256]{1,0:T(8,128)(2,1)S(1)}, bf16[128,256]{1,0:T(8,128)(2,1)S(1)}, u32[]{:S(2)}, u32[]{:S(2)}) collective-permute-start(bf16[128,256]{1,0:T(8,128)(2,1)S(1)} %get-tuple-element.769), channel_id=1, source_target_pairs={{4,0},{8,4},{12,8},{16,12},{20,16},{24,20},{28,24},{0,28},{5,1},{9... | collective-permute-start | bytes 196616 | tf_op jit(solution)/shard_map/while/body/eval_jaxpr/ppermute | solution.py:13
  52.4 4.8 %collective-permute-start.3 = (bf16[128,256]{1,0:T(8,128)(2,1)S(1)}, bf16[128,256]{1,0:T(8,128)(2,1)S(1)}, u32[]{:S(2)}, u32[]{:S(2)}) collective-permute-start(bf16[128,256]{1,0:T(8,128)(2,1)S(1)} %get-tuple-element.770), channel_id=1, source_target_pairs={{4,0},{8,4},{12,8},{16,12},{20,16},{24,20},{28,24},{0,28},{5,1},{9... | collective-permute-start | bytes 196616 | tf_op jit(solution)/shard_map/while/body/eval_jaxpr/ppermute | solution.py:13
  57.8 7.4 %collective-permute-start = (bf16[128,256]{1,0:T(8,128)(2,1)S(1)}, bf16[128,256]{1,0:T(8,128)(2,1)S(1)}, u32[]{:S(2)}, u32[]{:S(2)}) collective-permute-start(bf16[128,256]{1,0:T(8,128)(2,1)S(1)} %get-tuple-element.767), channel_id=1, source_target_pairs={{28,0},{0,4},{4,8},{8,12},{12,16},{16,20},{20,24},{24,28},{29,1},{... | collective-permute-start | bytes 196616 | tf_op jit(solution)/shard_map/while/body/eval_jaxpr/ppermute | solution.py:13
  57.9 9.1 %collective-permute-start.2 = (bf16[128,256]{1,0:T(8,128)(2,1)S(1)}, bf16[128,256]{1,0:T(8,128)(2,1)S(1)}, u32[]{:S(2)}, u32[]{:S(2)}) collective-permute-start(bf16[128,256]{1,0:T(8,128)(2,1)S(1)} %get-tuple-element.768), channel_id=1, source_target_pairs={{28,0},{0,4},{4,8},{8,12},{12,16},{16,20},{20,24},{24,28},{29,1},{... | collective-permute-start | bytes 196616 | tf_op jit(solution)/shard_map/while/body/eval_jaxpr/ppermute | solution.py:13
  58.6 8.1 %collective-permute-start.1 = (bf16[128,256]{1,0:T(8,128)(2,1)S(1)}, bf16[128,256]{1,0:T(8,128)(2,1)S(1)}, u32[]{:S(2)}, u32[]{:S(2)}) collective-permute-start(bf16[128,256]{1,0:T(8,128)(2,1)S(1)} %get-tuple-element.769), channel_id=1, source_target_pairs={{4,0},{8,4},{12,8},{16,12},{20,16},{24,20},{28,24},{0,28},{5,1},{9... | collective-permute-start | bytes 196616 | tf_op jit(solution)/shard_map/while/body/eval_jaxpr/ppermute | solution.py:13
  62.7 4.9 %collective-permute-start.3 = (bf16[128,256]{1,0:T(8,128)(2,1)S(1)}, bf16[128,256]{1,0:T(8,128)(2,1)S(1)}, u32[]{:S(2)}, u32[]{:S(2)}) collective-permute-start(bf16[128,256]{1,0:T(8,128)(2,1)S(1)} %get-tuple-element.770), channel_id=1, source_target_pairs={{4,0},{8,4},{12,8},{16,12},{20,16},{24,20},{28,24},{0,28},{5,1},{9... | collective-permute-start | bytes 196616 | tf_op jit(solution)/shard_map/while/body/eval_jaxpr/ppermute | solution.py:13
  68.2 7.4 %collective-permute-start = (bf16[128,256]{1,0:T(8,128)(2,1)S(1)}, bf16[128,256]{1,0:T(8,128)(2,1)S(1)}, u32[]{:S(2)}, u32[]{:S(2)}) collective-permute-start(bf16[128,256]{1,0:T(8,128)(2,1)S(1)} %get-tuple-element.767), channel_id=1, source_target_pairs={{28,0},{0,4},{4,8},{8,12},{12,16},{16,20},{20,24},{24,28},{29,1},{... | collective-permute-start | bytes 196616 | tf_op jit(solution)/shard_map/while/body/eval_jaxpr/ppermute | solution.py:13
  68.2 9.2 %collective-permute-start.2 = (bf16[128,256]{1,0:T(8,128)(2,1)S(1)}, bf16[128,256]{1,0:T(8,128)(2,1)S(1)}, u32[]{:S(2)}, u32[]{:S(2)}) collective-permute-start(bf16[128,256]{1,0:T(8,128)(2,1)S(1)} %get-tuple-element.768), channel_id=1, source_target_pairs={{28,0},{0,4},{4,8},{8,12},{12,16},{16,20},{20,24},{24,28},{29,1},{... | collective-permute-start | bytes 196616 | tf_op jit(solution)/shard_map/while/body/eval_jaxpr/ppermute | solution.py:13
  69.0 8.1 %collective-permute-start.1 = (bf16[128,256]{1,0:T(8,128)(2,1)S(1)}, bf16[128,256]{1,0:T(8,128)(2,1)S(1)}, u32[]{:S(2)}, u32[]{:S(2)}) collective-permute-start(bf16[128,256]{1,0:T(8,128)(2,1)S(1)} %get-tuple-element.769), channel_id=1, source_target_pairs={{4,0},{8,4},{12,8},{16,12},{20,16},{24,20},{28,24},{0,28},{5,1},{9... | collective-permute-start | bytes 196616 | tf_op jit(solution)/shard_map/while/body/eval_jaxpr/ppermute | solution.py:13
  73.0 5.0 %collective-permute-start.3 = (bf16[128,256]{1,0:T(8,128)(2,1)S(1)}, bf16[128,256]{1,0:T(8,128)(2,1)S(1)}, u32[]{:S(2)}, u32[]{:S(2)}) collective-permute-start(bf16[128,256]{1,0:T(8,128)(2,1)S(1)} %get-tuple-element.770), channel_id=1, source_target_pairs={{4,0},{8,4},{12,8},{16,12},{20,16},{24,20},{28,24},{0,28},{5,1},{9... | collective-permute-start | bytes 196616 | tf_op jit(solution)/shard_map/while/body/eval_jaxpr/ppermute | solution.py:13
  79.9 9.4 %all-to-all-start = ((bf16[4,32,1024]{2,1,0:T(8,128)(2,1)}), bf16[4,32,1024]{2,1,0:T(8,128)(2,1)S(1)}, u32[]{:S(2)}, u32[]{:S(2)}) async-start(bf16[4,32,1024]{2,1,0:T(8,128)(2,1)} %convert_element_type.34), calls=%async_computation | async-start | bytes 524288 | tf_op jit(solution)/shard_map/all_to_all | solution.py:111
  (1 other events, 0.7 us)
where the time goes:
time: 90.2 us; the launch traced here: 90 us
  starting transfers between devices  52.3 us (58%)
  waiting for transfers between devices  17.4 us (19%)
  matrix products  7.57 us (8%)
  local copies, waits for them, and re-layouts  6.75 us (7%)
  other arithmetic  4.34 us (5%)
    ppermute x28, starting transfers between devices, passed_along(): return lax.ppermute(block, axis, route)  48.9 us
    ppermute x28, waiting for transfers between devices, passed_along(): return lax.ppermute(block, axis, route)  12 us
    all_to_all x1, waiting for transfers between devices, local(): lax.all_to_all(output, 'head', split_axis=0, concat_axis=1, tiled=True)  5.38 us
    dot_general x15, matrix products, attend(): jnp.einsum('hgqk,khd->qhgd', weights.astype(jnp.bfloat16), values, prefer...  4.25 us
    all_to_all x1, starting transfers between devices, local(): lax.all_to_all(output, 'head', split_axis=0, concat_axis=1, tiled=True)  3.41 us
    dot_general x15, matrix products, attend(): jnp.einsum('qhgd,khd->hgqk', queries, keys, preferred_element_type=jnp.fl...  3.32 us
    unnamed x10, local copies, waits for them, and re-layouts  1.87 us
  transfers between devices with their start and end apart: 29, of which 14 were waited for; matrix products, arithmetic and copies ran while one was open for 10% of the time, Pallas kernels for 0%

commit v1 on v0

v1 whole, which is shorter than its diff:
```python
import functools

import jax
import jax.numpy as jnp
from jax import lax
from jax.experimental import pallas as pl
from jax.experimental.pallas import tpu as pltpu
from jax.sharding import PartitionSpec as P

HEAD_SIZE = 256
QUERY_GROUP = 2
MASKED = -1e30
FLOOR = -1e20
MESH = pl.DeviceIdType.MESH


def loop(first, last, body):
    if last - first <= 8:
        for i in range(first, last):
            body(i)
    else:
        lax.fori_loop(first, last, lambda i, c: (body(i), c)[1], 0)


def kernel(
    n, nh, order, q_hbm, k_hbm, v_hbm, attn, lse,
    qbuf, qout, kvown, kvbuf, maxima, sums, accum, obuf, lse_tx, lse_rx,
    load_sem, z_send, y_send, kv_recv, q_sem, o_send, o_recv, l_sem,
):
    head_dim, group = HEAD_SIZE, QUERY_GROUP
    rows = k_hbm.shape[0]
    keep = rows // nh
    line = n // 2
    scale = head_dim ** (-0.5)
    me, h = lax.axis_index("seq"), lax.axis_index("head")
    p, y = me // 2, lax.rem(me, 2)
    mine = lax.rem(p, 2)
    mate_p = p + 1 - 2 * mine
    mate = mate_p * 2 + y
    across = p * 2 + 1 - y
    width = group * head_dim

    def far(k):
        if isinstance(k, int):
            q, bit = 0, 1
            while bit < line:
                b = lax.rem(p // bit, 2)
                q = q + bit * ((1 - b) if k & bit else b)
                bit *= 2
            return q
        q, bit = 0, 1
        while bit < line:
            b, c = lax.rem(p // bit, 2), lax.rem(k // bit, 2)
            q = q + bit * lax.rem(b + c, 2)
            bit *= 2
        return q

    def lanes(start, size):
        return pl.ds(pl.multiple_of(start, head_dim), size)

    loads = []

    def load(src, dst):
        c = pltpu.make_async_copy(src, dst, load_sem.at[len(loads)])
        c.start()
        loads.append(c)

    for i, src in enumerate((k_hbm, v_hbm)):
        load(src.at[:, lanes(mine * head_dim, head_dim)], kvbuf.at[me, i])
    for j in range(2):
        for i, src in enumerate((k_hbm, v_hbm)):
            load(src.at[:, lanes(j * head_dim, head_dim)], kvown.at[j, i])
    for g in range(group):
        load(q_hbm.at[:, lanes(((1 - mine) * group + g) * head_dim, head_dim)],
             qout.at[pl.ds(g * rows, rows)])
    for g in range(group):
        load(q_hbm.at[:, lanes((mine * group + g) * head_dim, head_dim)],
             qbuf.at[0, pl.ds(g * rows, rows)])

    barrier = pltpu.get_barrier_semaphore()

    def greet(s, hh):
        pl.semaphore_signal(barrier, inc=1, device_id=(s, hh), device_id_type=MESH)

    greet(across, h)
    loop(1, line, lambda k: greet(far(k) * 2 + y, h))
    for j in range(1, nh):
        greet(me, lax.rem(h + j, nh))
        greet(mate, lax.rem(h + j, nh))

    maxima[...] = jnp.full_like(maxima, FLOOR)
    sums[...] = jnp.zeros_like(sums)
    accum[...] = jnp.zeros_like(accum)

    pl.semaphore_wait(barrier, 1 + (line - 1) + 2 * (nh - 1))

    def y_copy(q):
        slot = q * 2 + y
        return pltpu.make_async_remote_copy(
            src_ref=kvbuf.at[slot], dst_ref=kvbuf.at[slot],
            send_sem=y_send.at[q], recv_sem=kv_recv.at[slot],
            device_id=(across, h), device_id_type=MESH)

    def z_copy(k):
        q = far(k)
        return pltpu.make_async_remote_copy(
            src_ref=kvown.at[lax.rem(q, 2)], dst_ref=kvbuf.at[me],
            send_sem=z_send.at[k], recv_sem=kv_recv.at[me],
            device_id=(q * 2 + y, h), device_id_type=MESH)

    def arrived(slot):
        pltpu.make_async_remote_copy(
            src_ref=kvbuf.at[slot], dst_ref=kvbuf.at[slot],
            send_sem=y_send.at[0], recv_sem=kv_recv.at[slot],
            device_id=(across, h), device_id_type=MESH).wait_recv()

    q_copy = pltpu.make_async_remote_copy(
        src_ref=qout, dst_ref=qbuf.at[1], send_sem=q_sem.at[0], recv_sem=q_sem.at[1],
        device_id=(mate, h), device_id_type=MESH)

    for c in loads[:2]:
        c.wait()
    y_copy(p).start()
    for c in loads[2:6]:
        c.wait()
    loop(1, line, lambda k: z_copy(line - k).start())
    for c in loads[6:]:
        c.wait()
    q_copy.start()

    row = lax.broadcasted_iota(jnp.int32, (rows, rows), 0)
    col = lax.broadcasted_iota(jnp.int32, (rows, rows), 1)
    per = order.shape[0] // n
    blk = rows // per

    def placed(index, s):
        out = index + order[s * per] * blk
        for b in range(1, per):
            out = jnp.where(index >= b * blk, index + (order[s * per + b] - b) * blk, out)
        return out

    query_pos = [placed(row, s) for s in (me, mate)]

    def attend(rs, slot):
        keys, values = kvbuf[slot, 0], kvbuf[slot, 1]
        scores = lax.dot_general(
            qbuf[rs], keys, (((1,), (1,)), ((), ())), preferred_element_type=jnp.float32) * scale
        allowed = placed(col, slot) <= query_pos[rs]
        scores = jnp.where(jnp.concatenate([allowed] * group, 0), scores, MASKED)
        before = maxima[rs]
        fresh = jnp.maximum(before, jnp.max(scores, axis=1, keepdims=True))
        weights = jnp.exp(scores - fresh)
        factor = jnp.exp(before - fresh)
        maxima[rs] = fresh
        sums[rs] = sums[rs] * factor + weights
        update = lax.dot_general(
            weights.astype(jnp.bfloat16), values, (((1,), (0,)), ((), ())),
            preferred_element_type=jnp.float32)
        accum[rs] = accum[rs] * jnp.concatenate([factor] * (head_dim // rows), 1) + update

    attend(0, me)
    arrived(across)
    attend(0, across)

    def step(k):
        q = far(line - k)
        slot = q * 2 + y
        arrived(slot)
        y_copy(q).start()
        attend(0, slot)

    def step_with_last(k):
        step(k)
        last = far(line - k + 1) * 2 + 1 - y
        arrived(last)
        attend(0, last)

    step(1)
    loop(2, line, step_with_last)
    q_copy.wait_recv()
    final = far(1) * 2 + 1 - y
    attend(1, me)
    attend(1, across)

    def catch_up(k):
        q = far(line - k)
        attend(1, q * 2 + y)
        attend(1, q * 2 + 1 - y)

    loop(1, line - 1, catch_up)
    attend(1, far(1) * 2 + y)
    arrived(final)

    def finish(rs):
        attend(rs, final)
        total = jnp.sum(sums[rs], axis=1, keepdims=True)
        out = (accum[rs] / total).astype(jnp.bfloat16)
        for g in range(group):
            obuf[rs, :, g * head_dim:(g + 1) * head_dim] = out[g * rows:(g + 1) * rows]
        return jnp.log(total) + maxima[rs]

    def put_lse(rs, full):
        for g in range(group):
            lse_tx[rs, g:g + 1, :] = jnp.transpose(full[g * rows:(g + 1) * rows])[:1]

    columns = lanes((h * 2 + mine) * width, width)

    def o_copy(rs, j):
        to = lax.rem(h + j, nh)
        return pltpu.make_async_remote_copy(
            src_ref=obuf.at[rs, pl.ds(pl.multiple_of(to * keep, keep), keep)],
            dst_ref=attn.at[:, columns],
            send_sem=o_send.at[rs, j], recv_sem=o_recv.at[rs, h],
            device_id=((me, mate)[rs], to), device_id_type=MESH)

    outs = []
    full = finish(1)
    for j in range(nh):
        outs.append(o_copy(1, j))
        outs[-1].start()
    put_lse(1, full)
    lse_copy = pltpu.make_async_remote_copy(
        src_ref=lse_tx.at[1], dst_ref=lse_rx, send_sem=l_sem.at[0], recv_sem=l_sem.at[1],
        device_id=(mate, h), device_id_type=MESH)
    lse_copy.start()
    full = finish(0)
    for j in range(1, nh):
        outs.append(o_copy(0, j))
        outs[-1].start()
    kept = pltpu.make_async_copy(
        obuf.at[0, pl.ds(pl.multiple_of(h * keep, keep), keep)], attn.at[:, columns],
        o_send.at[0, 0])
    kept.start()
    put_lse(0, full)

    lse_copy.wait_recv()
    own, other = lse_tx[0, :group], lse_rx[:group]
    low = jnp.where(mine == 0, own, other)
    high = jnp.where(mine == 0, other, own)
    lse[...] = jnp.concatenate([low, high], 0)

    for rs in range(2):
        for j in range(1 - rs, nh):
            source = lax.rem(h + j, nh)
            spot = lanes((source * 2 + (mine, 1 - mine)[rs]) * width, width)
            pltpu.make_async_remote_copy(
                src_ref=obuf.at[rs, pl.ds(0, keep)], dst_ref=attn.at[:, spot],
                send_sem=o_send.at[rs, j], recv_sem=o_recv.at[rs, source],
                device_id=(mate, h), device_id_type=MESH).wait_recv()
    kept.wait()
    for c in outs:
        c.wait_send()
    lse_copy.wait_send()
    q_copy.wait_send()
    y_copy(p).wait_send()
    loop(1, line, lambda k: (z_copy(k).wait_send(), y_copy(far(k)).wait_send()))


def local(n, nh, queries, keys, values, block_order):
    rows = queries.shape[0]
    head_dim, group = HEAD_SIZE, QUERY_GROUP
    line = n // 2
    high = group * rows
    bf16, f32 = jnp.bfloat16, jnp.float32
    dma = pltpu.SemaphoreType.DMA
    return pl.pallas_call(
        functools.partial(kernel, n, nh),
        out_shape=(
            jax.ShapeDtypeStruct((rows // nh, queries.shape[1] * nh), bf16),
            jax.ShapeDtypeStruct((2 * group, rows), f32),
        ),
        in_specs=[pl.BlockSpec(memory_space=pltpu.SMEM)] + [pl.BlockSpec(memory_space=pl.ANY)] * 3,
        out_specs=(pl.BlockSpec(memory_space=pl.ANY), pl.BlockSpec(memory_space=pltpu.VMEM)),
        scratch_shapes=[
            pltpu.VMEM((2, high, head_dim), bf16),
            pltpu.VMEM((high, head_dim), bf16),
            pltpu.VMEM((2, 2, rows, head_dim), bf16),
            pltpu.VMEM((n, 2, rows, head_dim), bf16),
            pltpu.VMEM((2, high, rows), f32),
            pltpu.VMEM((2, high, rows), f32),
            pltpu.VMEM((2, high, head_dim), f32),
            pltpu.VMEM((2, rows, group * head_dim), bf16),
            pltpu.VMEM((2, 8, rows), f32),
            pltpu.VMEM((8, rows), f32),
            dma((6 + 2 * group,)),
            dma((line,)),
            dma((line,)),
            dma((n,)),
            dma((2,)),
            dma((2, nh)),
            dma((2, nh)),
            dma((2,)),
        ],
        compiler_params=pltpu.CompilerParams(collective_id=0, has_side_effects=True),
    )(block_order, queries, keys, values)


def solution(mesh):
    in_specs = (P("seq", "head"), P("seq", "head"), P("seq", "head"), P())
    out_specs = (P(("seq", "head"), None), P("head", "seq"))
    body = functools.partial(local, mesh.shape["seq"], mesh.shape["head"])
    return jax.shard_map(body, mesh=mesh, in_specs=in_specs, out_specs=out_specs, check_vma=False)
```

time: 90.2 us -> 35.9 us (0.40)
  starting transfers between devices: 52.3 us -> 0 us
  Pallas kernels: 0 us -> 32.8 us
  waiting for transfers between devices: 17.4 us -> 0 us
  matrix products: 7.57 us -> 0 us
  local copies, waits for them, and re-layouts: 6.75 us -> 2.25 us
  other arithmetic: 4.34 us -> 0 us
    ppermute x28 -> x0, starting transfers between devices: 48.9 us -> none  [passed_along(): return lax.ppermute(block, axis, route)]
    pallas_call x0 -> x1, Pallas kernels: none -> 32.8 us  [local(): pl.pallas_call(functools.partial(kernel, n, nh), out_shape=(jax.ShapeDtyp...]
    ppermute x28 -> x0, waiting for transfers between devices: 12 us -> none  [passed_along(): return lax.ppermute(block, axis, route)]
    dot_general x30 -> x0, matrix products: 7.57 us -> none  [the longest x15 4.25 us: attend(): jnp.einsum('hgqk,khd->qhgd', weights.astype(jnp.bfloat16), values, prefer...]
    all_to_all x1 -> x0, waiting for transfers between devices: 5.38 us -> none  [local(): lax.all_to_all(output, 'head', split_axis=0, concat_axis=1, tiled=True)]
    all_to_all x1 -> x0, starting transfers between devices: 3.41 us -> none  [local(): lax.all_to_all(output, 'head', split_axis=0, concat_axis=1, tiled=True)]
    add x16 -> x0, other arithmetic: 1.67 us -> none  [the longest x15 1.08 us: positions(): ids[:, None] * blk + jnp.arange(blk, dtype=jnp.int32)[None, :]]
    add x15 -> x0, local copies, waits for them, and re-layouts: 1.23 us -> none  [positions(): ids[:, None] * blk + jnp.arange(blk, dtype=jnp.int32)[None, :]]
  transfers between devices with their start and end apart: 29 -> 0, of which waited for: 14 -> 0; matrix products, arithmetic and copies ran while one was open for 10% -> 0% of each run, Pallas kernels for 0% -> 0%
where the time goes in v1:
time: 35.9 us; the launch traced here: 35.7 us
  Pallas kernels  32.8 us (91%)
  local copies, waits for them, and re-layouts  2.25 us (6%)
  between operations  0.65 us (2%)
    pallas_call x1, Pallas kernels, local(): pl.pallas_call(functools.partial(kernel, n, nh), out_shape=(jax.ShapeDtyp...  32.8 us
    unnamed x4, local copies, waits for them, and re-layouts  2.25 us

profile of v1, /device:TPU:0, one launch (start us, length us, event | category | flops | bytes accessed | tf_op | source)
XLA Modules:
  0.0 35.7 jit_solution(14512133232127372766)
XLA Ops:
  0.6 32.8 %shard_map.59 = (bf16[32,4096]{1,0:T(8,128)(2,1)}, f32[4,128]{1,0:T(4,128)}) custom-call(s32[16]{0:T(128)} %order.1, bf16[128,1024]{1,0:T(8,128)(2,1)} %q_hbm.1, bf16[128,512]{1,0:T(8,128)(2,1)} %k_hbm.1, bf16[128,512]{1,0:T(8,128)(2,1)} %v_hbm.1), custom_call_target="tpu_custom_call" | custom-call | tf_op jit(solution)/shard_map/pallas_call | solution.py:266
  33.4 0.0 copy-start
  33.4 1.7 %copy.8 = bf16[32,4096]{1,0:T(8,128)(2,1)} copy(bf16[32,4096]{1,0:T(8,128)(2,1)} %get-tuple-element.4) | data formatting | bytes 524288
  35.1 0.0 copy-done
  35.1 0.6 %copy.9 = f32[4,128]{1,0:T(4,128)} copy(f32[4,128]{1,0:T(4,128)S(1)} %copy-done) | data formatting | bytes 4096
Async XLA Ops:
  33.4 1.7 %copy-start = (f32[4,128]{1,0:T(4,128)S(1)}, f32[4,128]{1,0:T(4,128)}, u32[]{:S(2)}) copy-start(f32[4,128]{1,0:T(4,128)} %get-tuple-element.5) | copy-start | bytes 6148

commit v2 on v1

--- a/solution.py
+++ b/solution.py
@@ -11,6 +11,7 @@
 QUERY_GROUP = 2
 MASKED = -1e30
 FLOOR = -1e20
+PARTS = 2
 MESH = pl.DeviceIdType.MESH
 
 
@@ -30,6 +31,7 @@
     head_dim, group = HEAD_SIZE, QUERY_GROUP
     rows = k_hbm.shape[0]
     keep = rows // nh
+    part = rows // PARTS
     line = n // 2
     scale = head_dim ** (-0.5)
     me, h = lax.axis_index("seq"), lax.axis_index("head")
@@ -40,20 +42,18 @@
     across = p * 2 + 1 - y
     width = group * head_dim
 
+    core = lax.rem(h, 2)
+
     def far(k):
-        if isinstance(k, int):
-            q, bit = 0, 1
-            while bit < line:
-                b = lax.rem(p // bit, 2)
-                q = q + bit * ((1 - b) if k & bit else b)
-                bit *= 2
-            return q
         q, bit = 0, 1
         while bit < line:
-            b, c = lax.rem(p // bit, 2), lax.rem(k // bit, 2)
-            q = q + bit * lax.rem(b + c, 2)
+            b, c = lax.rem(p // bit, 2), (k // bit) % 2
+            q = q + bit * (b + c - 2 * b * c)
             bit *= 2
         return q
+
+    def turn(i):
+        return jnp.where(core == 0, line - i, jnp.where(jnp.int32(i) == 1, 1, line - i + 1))
 
     def lanes(start, size):
         return pl.ds(pl.multiple_of(start, head_dim), size)
@@ -66,10 +66,14 @@
         loads.append(c)
 
     for i, src in enumerate((k_hbm, v_hbm)):
-        load(src.at[:, lanes(mine * head_dim, head_dim)], kvbuf.at[me, i])
+        for t in range(PARTS):
+            load(src.at[pl.ds(t * part, part), lanes(mine * head_dim, head_dim)],
+                 kvbuf.at[me, t, i])
     for j in range(2):
         for i, src in enumerate((k_hbm, v_hbm)):
-            load(src.at[:, lanes(j * head_dim, head_dim)], kvown.at[j, i])
+            for t in range(PARTS):
+                load(src.at[pl.ds(t * part, part), lanes(j * head_dim, head_dim)],
+                     kvown.at[j, t, i])
     for g in range(group):
         load(q_hbm.at[:, lanes(((1 - mine) * group + g) * head_dim, head_dim)],
              qout.at[pl.ds(g * rows, rows)])
@@ -94,39 +98,56 @@
 
     pl.semaphore_wait(barrier, 1 + (line - 1) + 2 * (nh - 1))
 
-    def y_copy(q):
+    def y_copy(q, t):
         slot = q * 2 + y
         return pltpu.make_async_remote_copy(
-            src_ref=kvbuf.at[slot], dst_ref=kvbuf.at[slot],
-            send_sem=y_send.at[q], recv_sem=kv_recv.at[slot],
+            src_ref=kvbuf.at[slot, t], dst_ref=kvbuf.at[slot, t],
+            send_sem=y_send.at[q, t], recv_sem=kv_recv.at[slot, t],
             device_id=(across, h), device_id_type=MESH)
 
-    def z_copy(k):
+    def z_copy(k, t):
         q = far(k)
         return pltpu.make_async_remote_copy(
-            src_ref=kvown.at[lax.rem(q, 2)], dst_ref=kvbuf.at[me],
-            send_sem=z_send.at[k], recv_sem=kv_recv.at[me],
+            src_ref=kvown.at[lax.rem(q, 2), t], dst_ref=kvbuf.at[me, t],
+            send_sem=z_send.at[k, t], recv_sem=kv_recv.at[me, t],
             device_id=(q * 2 + y, h), device_id_type=MESH)
 
+    def landed(slot, t):
+        pltpu.make_async_remote_copy(
+            src_ref=kvbuf.at[slot, t], dst_ref=kvbuf.at[slot, t],
+            send_sem=y_send.at[0, t], recv_sem=kv_recv.at[slot, t],
+            device_id=(across, h), device_id_type=MESH).wait_recv()
+
     def arrived(slot):
-        pltpu.make_async_remote_copy(
-            src_ref=kvbuf.at[slot], dst_ref=kvbuf.at[slot],
-            send_sem=y_send.at[0], recv_sem=kv_recv.at[slot],
-            device_id=(across, h), device_id_type=MESH).wait_recv()
+        for t in range(PARTS):
+            landed(slot, t)
 
     q_copy = pltpu.make_async_remote_copy(
         src_ref=qout, dst_ref=qbuf.at[1], send_sem=q_sem.at[0], recv_sem=q_sem.at[1],
         device_id=(mate, h), device_id_type=MESH)
 
-    for c in loads[:2]:
+    for c in loads[:2 * PARTS]:
         c.wait()
-    y_copy(p).start()
-    for c in loads[2:6]:
+    for t in range(PARTS):
+        y_copy(p, t).start()
+    for c in loads[2 * PARTS:]:
         c.wait()
-    loop(1, line, lambda k: z_copy(line - k).start())
-    for c in loads[6:]:
-        c.wait()
-    q_copy.start()
+
+    def send(i):
+        for t in range(PARTS):
+            z_copy(turn(i), t).start()
+
+    send(1)
+
+    @pl.when(core == 1)
+    def _():
+        q_copy.start()
+
+    loop(2, line, send)
+
+    @pl.when(core == 0)
+    def _():
+        q_copy.start()
 
     row = lax.broadcasted_iota(jnp.int32, (rows, rows), 0)
     col = lax.broadcasted_iota(jnp.int32, (rows, rows), 1)
@@ -142,7 +163,8 @@
     query_pos = [placed(row, s) for s in (me, mate)]
 
     def attend(rs, slot):
-        keys, values = kvbuf[slot, 0], kvbuf[slot, 1]
+        keys, values = kvbuf[slot, :, 0], kvbuf[slot, :, 1]
+        keys, values = (z.reshape(rows, head_dim) for z in (keys, values))
         scores = lax.dot_general(
             qbuf[rs], keys, (((1,), (1,)), ((), ())), preferred_element_type=jnp.float32) * scale
         allowed = placed(col, slot) <= query_pos[rs]
@@ -162,33 +184,35 @@
     arrived(across)
     attend(0, across)
 
-    def step(k):
-        q = far(line - k)
+    def step(i):
+        q = far(turn(i))
         slot = q * 2 + y
-        arrived(slot)
-        y_copy(q).start()
+        for t in range(PARTS):
+            landed(slot, t)
+            y_copy(q, t).start()
         attend(0, slot)
 
-    def step_with_last(k):
-        step(k)
-        last = far(line - k + 1) * 2 + 1 - y
+    def step_with_last(i):
+        step(i)
+        last = far(turn(i - 1)) * 2 + 1 - y
         arrived(last)
         attend(0, last)
 
     step(1)
     loop(2, line, step_with_last)
     q_copy.wait_recv()
-    final = far(1) * 2 + 1 - y
     attend(1, me)
     attend(1, across)
 
-    def catch_up(k):
-        q = far(line - k)
+    def catch_up(i):
+        q = far(turn(i))
         attend(1, q * 2 + y)
         attend(1, q * 2 + 1 - y)
 
     loop(1, line - 1, catch_up)
-    attend(1, far(1) * 2 + y)
+    end = far(turn(line - 1))
+    attend(1, end * 2 + y)
+    final = end * 2 + 1 - y
     arrived(final)
 
     def finish(rs):
@@ -252,8 +276,9 @@
         c.wait_send()
     lse_copy.wait_send()
     q_copy.wait_send()
-    y_copy(p).wait_send()
-    loop(1, line, lambda k: (z_copy(k).wait_send(), y_copy(far(k)).wait_send()))
+    for t in range(PARTS):
+        y_copy(p, t).wait_send()
+        loop(1, line, lambda k: (z_copy(k, t).wait_send(), y_copy(far(k), t).wait_send()))
 
 
 def local(n, nh, queries, keys, values, block_order):
@@ -269,23 +294,23 @@
             jax.ShapeDtypeStruct((rows // nh, queries.shape[1] * nh), bf16),
             jax.ShapeDtypeStruct((2 * group, rows), f32),
         ),
-        in_specs=[pl.BlockSpec(memory_space=pltpu.SMEM)] + [pl.BlockSpec(memory_space=pl.ANY)] * 3,
+        in_specs=[pl.BlockSpec(memory_space=pltpu.SMEM)] + [pl.BlockSpec(memory_space=pltpu.MemorySpace.HBM)] * 3,
         out_specs=(pl.BlockSpec(memory_space=pl.ANY), pl.BlockSpec(memory_space=pltpu.VMEM)),
         scratch_shapes=[
             pltpu.VMEM((2, high, head_dim), bf16),
             pltpu.VMEM((high, head_dim), bf16),
-            pltpu.VMEM((2, 2, rows, head_dim), bf16),
-            pltpu.VMEM((n, 2, rows, head_dim), bf16),
+            pltpu.VMEM((2, PARTS, 2, rows // PARTS, head_dim), bf16),
+            pltpu.VMEM((n, PARTS, 2, rows // PARTS, head_dim), bf16),
             pltpu.VMEM((2, high, rows), f32),
             pltpu.VMEM((2, high, rows), f32),
             pltpu.VMEM((2, high, head_dim), f32),
             pltpu.VMEM((2, rows, group * head_dim), bf16),
             pltpu.VMEM((2, 8, rows), f32),
             pltpu.VMEM((8, rows), f32),
-            dma((6 + 2 * group,)),
-            dma((line,)),
-            dma((line,)),
-            dma((n,)),
+            dma((6 * PARTS + 2 * group,)),
+            dma((line, PARTS)),
+            dma((line, PARTS)),
+            dma((n, PARTS)),
             dma((2,)),
             dma((2, nh)),
             dma((2, nh)),

time: 35.9 us -> 32.7 us (0.911)
  Pallas kernels: 32.8 us -> 29.7 us
    pallas_call x1, Pallas kernels: 32.8 us -> 29.7 us  [local(): pl.pallas_call(functools.partial(kernel, n, nh), out_shape=(jax.ShapeDtyp...]
where the time goes in v2:
time: 32.7 us; the launch traced here: 32.6 us
  Pallas kernels  29.7 us (91%)
  local copies, waits for them, and re-layouts  2.25 us (7%)
  between operations  0.65 us (2%)
    pallas_call x1, Pallas kernels, local(): pl.pallas_call(functools.partial(kernel, n, nh), out_shape=(jax.ShapeDtyp...  29.7 us
    unnamed x4, local copies, waits for them, and re-layouts  2.25 us

profile of v2, /device:TPU:0, one launch (start us, length us, event | category | flops | bytes accessed | tf_op | source)
XLA Modules:
  0.0 32.6 jit_solution(3058590897559056815)
XLA Ops:
  0.6 29.7 %shard_map.59 = (bf16[32,4096]{1,0:T(8,128)(2,1)}, f32[4,128]{1,0:T(4,128)}) custom-call(s32[16]{0:T(128)} %order.1, bf16[128,1024]{1,0:T(8,128)(2,1)} %q_hbm.1, bf16[128,512]{1,0:T(8,128)(2,1)} %k_hbm.1, bf16[128,512]{1,0:T(8,128)(2,1)} %v_hbm.1), custom_call_target="tpu_custom_call" | custom-call | tf_op jit(solution)/shard_map/pallas_call | solution.py:291
  30.3 0.0 copy-start
  30.3 1.7 %copy.8 = bf16[32,4096]{1,0:T(8,128)(2,1)} copy(bf16[32,4096]{1,0:T(8,128)(2,1)} %get-tuple-element.4) | data formatting | bytes 524288
  32.0 0.0 copy-done
  32.0 0.6 %copy.9 = f32[4,128]{1,0:T(4,128)} copy(f32[4,128]{1,0:T(4,128)S(1)} %copy-done) | data formatting | bytes 4096
Async XLA Ops:
  30.3 1.7 %copy-start = (f32[4,128]{1,0:T(4,128)S(1)}, f32[4,128]{1,0:T(4,128)}, u32[]{:S(2)}) copy-start(f32[4,128]{1,0:T(4,128)} %get-tuple-element.5) | copy-start | bytes 6148

commit v3 on v2

--- a/solution.py
+++ b/solution.py
@@ -24,8 +24,8 @@
 
 
 def kernel(
-    n, nh, order, q_hbm, k_hbm, v_hbm, attn, lse,
-    qbuf, qout, kvown, kvbuf, maxima, sums, accum, obuf, lse_tx, lse_rx,
+    n, nh, order_hbm, q_hbm, k_hbm, v_hbm, attn, lse,
+    qbuf, qout, kvown, kvbuf, maxima, sums, accum, obuf, lse_tx, lse_rx, lse_all, order,
     load_sem, z_send, y_send, kv_recv, q_sem, o_send, o_recv, l_sem,
 ):
     head_dim, group = HEAD_SIZE, QUERY_GROUP
@@ -53,7 +53,10 @@
         return q
 
     def turn(i):
-        return jnp.where(core == 0, line - i, jnp.where(jnp.int32(i) == 1, 1, line - i + 1))
+        i = jnp.int32(i)
+        second = jnp.where(i == 1, line - 1, jnp.where(i == 2, 1, line - i + 1))
+        first = jnp.where(i == 1, 1, line - i + 1)
+        return jnp.where(core == 0, second, first)
 
     def lanes(start, size):
         return pl.ds(pl.multiple_of(start, head_dim), size)
@@ -80,6 +83,8 @@
     for g in range(group):
         load(q_hbm.at[:, lanes((mine * group + g) * head_dim, head_dim)],
              qbuf.at[0, pl.ds(g * rows, rows)])
+
+    load(order_hbm, order)
 
     barrier = pltpu.get_barrier_semaphore()
 
@@ -261,7 +266,9 @@
     own, other = lse_tx[0, :group], lse_rx[:group]
     low = jnp.where(mine == 0, own, other)
     high = jnp.where(mine == 0, other, own)
-    lse[...] = jnp.concatenate([low, high], 0)
+    lse_all[...] = jnp.concatenate([low, high], 0)
+    lse_out = pltpu.make_async_copy(lse_all, lse, l_sem.at[2])
+    lse_out.start()
 
     for rs in range(2):
         for j in range(1 - rs, nh):
@@ -275,6 +282,7 @@
     for c in outs:
         c.wait_send()
     lse_copy.wait_send()
+    lse_out.wait()
     q_copy.wait_send()
     for t in range(PARTS):
         y_copy(p, t).wait_send()
@@ -294,8 +302,8 @@
             jax.ShapeDtypeStruct((rows // nh, queries.shape[1] * nh), bf16),
             jax.ShapeDtypeStruct((2 * group, rows), f32),
         ),
-        in_specs=[pl.BlockSpec(memory_space=pltpu.SMEM)] + [pl.BlockSpec(memory_space=pltpu.MemorySpace.HBM)] * 3,
-        out_specs=(pl.BlockSpec(memory_space=pl.ANY), pl.BlockSpec(memory_space=pltpu.VMEM)),
+        in_specs=[pl.BlockSpec(memory_space=pl.ANY)] * 4,
+        out_specs=(pl.BlockSpec(memory_space=pl.ANY),) * 2,
         scratch_shapes=[
             pltpu.VMEM((2, high, head_dim), bf16),
             pltpu.VMEM((high, head_dim), bf16),
@@ -307,14 +315,16 @@
             pltpu.VMEM((2, rows, group * head_dim), bf16),
             pltpu.VMEM((2, 8, rows), f32),
             pltpu.VMEM((8, rows), f32),
-            dma((6 * PARTS + 2 * group,)),
+            pltpu.VMEM((2 * group, rows), f32),
+            pltpu.SMEM(block_order.shape, jnp.int32),
+            dma((6 * PARTS + 2 * group + 1,)),
             dma((line, PARTS)),
             dma((line, PARTS)),
             dma((n, PARTS)),
             dma((2,)),
             dma((2, nh)),
             dma((2, nh)),
-            dma((2,)),
+            dma((3,)),
         ],
         compiler_params=pltpu.CompilerParams(collective_id=0, has_side_effects=True),
     )(block_order, queries, keys, values)

time: 32.7 us -> 30.8 us (0.942)
  Pallas kernels: 29.7 us -> 27.7 us
    pallas_call x1, Pallas kernels: 29.7 us -> 27.7 us  [local(): pl.pallas_call(functools.partial(kernel, n, nh), out_shape=(jax.ShapeDtyp...]
where the time goes in v3:
time: 30.8 us; the launch traced here: 30.6 us
  Pallas kernels  27.7 us (90%)
  local copies, waits for them, and re-layouts  2.25 us (7%)
  between operations  0.65 us (2%)
    pallas_call x1, Pallas kernels, local(): pl.pallas_call(functools.partial(kernel, n, nh), out_shape=(jax.ShapeDtyp...  27.7 us
    unnamed x4, local copies, waits for them, and re-layouts  2.25 us

profile of v3, /device:TPU:0, one launch (start us, length us, event | category | flops | bytes accessed | tf_op | source)
XLA Modules:
  0.0 30.6 jit_solution(8329596277151395265)
XLA Ops:
  0.6 27.7 %shard_map.59 = (bf16[32,4096]{1,0:T(8,128)(2,1)}, f32[4,128]{1,0:T(4,128)}) custom-call(s32[16]{0:T(128)} %order_hbm.1, bf16[128,1024]{1,0:T(8,128)(2,1)} %q_hbm.1, bf16[128,512]{1,0:T(8,128)(2,1)} %k_hbm.1, bf16[128,512]{1,0:T(8,128)(2,1)} %v_hbm.1), custom_call_target="tpu_custom_call" | custom-call | tf_op jit(solution)/shard_map/pallas_call | solution.py:299
  28.4 0.0 copy-start
  28.4 1.7 %copy.8 = bf16[32,4096]{1,0:T(8,128)(2,1)} copy(bf16[32,4096]{1,0:T(8,128)(2,1)} %get-tuple-element.4) | data formatting | bytes 524288
  30.1 0.0 copy-done
  30.1 0.6 %copy.9 = f32[4,128]{1,0:T(4,128)} copy(f32[4,128]{1,0:T(4,128)S(1)} %copy-done) | data formatting | bytes 4096
Async XLA Ops:
  28.4 1.7 %copy-start = (f32[4,128]{1,0:T(4,128)S(1)}, f32[4,128]{1,0:T(4,128)}, u32[]{:S(2)}) copy-start(f32[4,128]{1,0:T(4,128)} %get-tuple-element.5) | copy-start | bytes 6148

commit v4 on v3

--- a/solution.py
+++ b/solution.py
@@ -25,7 +25,7 @@
 
 def kernel(
     n, nh, order_hbm, q_hbm, k_hbm, v_hbm, attn, lse,
-    qbuf, qout, kvown, kvbuf, maxima, sums, accum, obuf, lse_tx, lse_rx, lse_all, order,
+    qbuf, qout, kvown, kvbuf, maxima, sums, accum, obuf, lse_tx, lse_rx, order,
     load_sem, z_send, y_send, kv_recv, q_sem, o_send, o_recv, l_sem,
 ):
     head_dim, group = HEAD_SIZE, QUERY_GROUP
@@ -55,8 +55,7 @@
     def turn(i):
         i = jnp.int32(i)
         second = jnp.where(i == 1, line - 1, jnp.where(i == 2, 1, line - i + 1))
-        first = jnp.where(i == 1, 1, line - i + 1)
-        return jnp.where(core == 0, second, first)
+        return jnp.where(core == 0, second, i)
 
     def lanes(start, size):
         return pl.ds(pl.multiple_of(start, head_dim), size)
@@ -266,9 +265,7 @@
     own, other = lse_tx[0, :group], lse_rx[:group]
     low = jnp.where(mine == 0, own, other)
     high = jnp.where(mine == 0, other, own)
-    lse_all[...] = jnp.concatenate([low, high], 0)
-    lse_out = pltpu.make_async_copy(lse_all, lse, l_sem.at[2])
-    lse_out.start()
+    lse[...] = jnp.concatenate([low, high], 0)
 
     for rs in range(2):
         for j in range(1 - rs, nh):
@@ -282,7 +279,6 @@
     for c in outs:
         c.wait_send()
     lse_copy.wait_send()
-    lse_out.wait()
     q_copy.wait_send()
     for t in range(PARTS):
         y_copy(p, t).wait_send()
@@ -299,11 +295,11 @@
     return pl.pallas_call(
         functools.partial(kernel, n, nh),
         out_shape=(
-            jax.ShapeDtypeStruct((rows // nh, queries.shape[1] * nh), bf16),
-            jax.ShapeDtypeStruct((2 * group, rows), f32),
+            pltpu.VMEM((rows // nh, queries.shape[1] * nh), bf16),
+            pltpu.VMEM((2 * group, rows), f32),
         ),
         in_specs=[pl.BlockSpec(memory_space=pl.ANY)] * 4,
-        out_specs=(pl.BlockSpec(memory_space=pl.ANY),) * 2,
+        out_specs=(pl.BlockSpec(memory_space=pltpu.VMEM),) * 2,
         scratch_shapes=[
             pltpu.VMEM((2, high, head_dim), bf16),
             pltpu.VMEM((high, head_dim), bf16),
@@ -315,7 +311,6 @@
             pltpu.VMEM((2, rows, group * head_dim), bf16),
             pltpu.VMEM((2, 8, rows), f32),
             pltpu.VMEM((8, rows), f32),
-            pltpu.VMEM((2 * group, rows), f32),
             pltpu.SMEM(block_order.shape, jnp.int32),
             dma((6 * PARTS + 2 * group + 1,)),
             dma((line, PARTS)),
@@ -324,7 +319,7 @@
             dma((2,)),
             dma((2, nh)),
             dma((2, nh)),
-            dma((3,)),
+            dma((2,)),
         ],
         compiler_params=pltpu.CompilerParams(collective_id=0, has_side_effects=True),
     )(block_order, queries, keys, values)

time: 30.8 us -> 29.4 us (0.955)
  local copies, waits for them, and re-layouts: 2.25 us -> 1.28 us
    unnamed x4 -> x2, local copies, waits for them, and re-layouts: 2.25 us -> 1.28 us
    pallas_call x1, Pallas kernels: 27.7 us -> 27.4 us  [local(): pl.pallas_call(functools.partial(kernel, n, nh), out_shape=(pltpu.VMEM((r...]
where the time goes in v4:
time: 29.4 us; the launch traced here: 29.3 us
  Pallas kernels  27.4 us (93%)
  local copies, waits for them, and re-layouts  1.28 us (4%)
  between operations  0.64 us (2%)
    pallas_call x1, Pallas kernels, local(): pl.pallas_call(functools.partial(kernel, n, nh), out_shape=(pltpu.VMEM((r...  27.4 us
    unnamed x2, local copies, waits for them, and re-layouts  1.28 us

profile of v4, /device:TPU:0, one launch (start us, length us, event | category | flops | bytes accessed | tf_op | source)
XLA Modules:
  0.0 29.3 jit_solution(5236477678512006048)
XLA Ops:
  0.6 27.4 %shard_map.59 = (bf16[32,4096]{1,0:T(8,128)(2,1)S(1)}, f32[4,128]{1,0:T(4,128)S(1)}) custom-call(s32[16]{0:T(128)} %order_hbm.1, bf16[128,1024]{1,0:T(8,128)(2,1)} %q_hbm.1, bf16[128,512]{1,0:T(8,128)(2,1)} %k_hbm.1, bf16[128,512]{1,0:T(8,128)(2,1)} %v_hbm.1), custom_call_target="tpu_custom_call" | custom-call | tf_op jit(solution)/shard_map/pallas_call | solution.py:295
  28.0 0.7 %copy.8 = bf16[32,4096]{1,0:T(8,128)(2,1)} copy(bf16[32,4096]{1,0:T(8,128)(2,1)S(1)} %get-tuple-element.2) | data formatting | bytes 524288
  28.7 0.6 %copy.9 = f32[4,128]{1,0:T(4,128)} copy(f32[4,128]{1,0:T(4,128)S(1)} %get-tuple-element.3) | data formatting | bytes 4096
